TPU v7x, 32 devices: a whole 2x2x4 slice. The times are simulated.
32 devices in a mesh: dp: 4 (over y, x), spatial: 8 (over z, core).
Axes of the slice: x: 2, y: 2, z: 4, core: 2. Of those that a mesh axis runs over, the one named last changes fastest.
Arguments:
- volume: bfloat16 [4, 16, 16, 8, 128], P('dp', 'spatial'), may hold values from -6 to 6
- cotangent: bfloat16 [4, 16, 16, 8, 128], P('dp', 'spatial'), may hold values from -6 to 6
- master: float32 [3456, 128], P('dp'), may hold values from -0.109375 to 0.109375
- moment: float32 [3456, 128], P('dp'), may hold values from -6 to 6
- second: float32 [3456, 128], P('dp'), may hold values from 0.25 to 4
Outputs:
- activation: bfloat16 [4, 16, 16, 8, 128], P('dp', 'spatial')
- input_grad: bfloat16 [4, 16, 16, 8, 128], P('dp', 'spatial')
- master_next: float32 [3456, 128], P('dp')
- moment_next: float32 [3456, 128], P('dp')
- second_next: float32 [3456, 128], P('dp')
All inputs are finite; a program needn't handle non-finite values.
Results may differ from a plain program's by a relative error of at most 0.002.
The roundings to bfloat16 on the way count: a program that leaves them out, or rounds other values in their place, can miss the bound.
Values may be sent and summed in bfloat16 or wider, within the bound.
A program may use at most 64 MiB of HBM per device.

v0:
```python
import math
import jax
import jax.numpy as jnp
from jax import lax
from jax.sharding import PartitionSpec as P


def with_halo(block, sides, width):
    for axis, dim in sides:
        count = lax.axis_size(axis)
        forward = [(i, i + 1) for i in range(count - 1)]
        backward = [(target, source) for source, target in forward]
        low = lax.ppermute(
            lax.slice_in_dim(block, block.shape[dim] - width, None, axis=dim), axis, forward
        )
        high = lax.ppermute(lax.slice_in_dim(block, 0, width, axis=dim), axis, backward)
        block = jnp.concatenate([low, block, high], axis=dim)
    return block


def silu_slope(preact):
    sigma = jax.nn.sigmoid(preact)
    return sigma * (1.0 + preact * (1.0 - sigma))


def pad_sides(field):
    return jnp.pad(field, ((0, 0), (1, 1), (1, 1), (0, 0)))


def forward_taps(padded, kernel, planes, rows, cols):
    width = kernel.shape[1]
    total = jnp.zeros((planes * rows * cols, width), jnp.float32)
    for offset_z in range(3):
        for offset_y in range(3):
            for offset_x in range(3):
                tap_index = offset_z * 9 + offset_y * 3 + offset_x
                piece = padded[
                    offset_z : offset_z + planes,
                    offset_y : offset_y + rows,
                    offset_x : offset_x + cols,
                ].reshape(-1, width)
                total = total + jnp.dot(
                    piece, kernel[tap_index], preferred_element_type=jnp.float32
                )
    return total


def backward_taps(grad_pad, kernel, planes, rows, cols):
    width = kernel.shape[1]
    total = jnp.zeros((planes * rows * cols, width), jnp.float32)
    for offset_z in range(3):
        for offset_y in range(3):
            for offset_x in range(3):
                tap_index = offset_z * 9 + offset_y * 3 + offset_x
                piece = grad_pad[
                    2 - offset_z : 2 - offset_z + planes,
                    2 - offset_y : 2 - offset_y + rows,
                    2 - offset_x : 2 - offset_x + cols,
                ].reshape(-1, width)
                total = total + lax.dot_general(
                    piece,
                    kernel[tap_index],
                    (((1,), (1,)), ((), ())),
                    preferred_element_type=jnp.float32,
                )
    return total


def weight_taps(padded, hidden_grad, planes, rows, cols):
    width = hidden_grad.shape[1]
    blocks = []
    for offset_z in range(3):
        for offset_y in range(3):
            for offset_x in range(3):
                piece = padded[
                    offset_z : offset_z + planes,
                    offset_y : offset_y + rows,
                    offset_x : offset_x + cols,
                ].reshape(-1, width)
                blocks.append(
                    lax.dot_general(
                        piece,
                        hidden_grad,
                        (((0,), (0,)), ((), ())),
                        preferred_element_type=jnp.float32,
                    )
                )
    return jnp.concatenate(blocks, axis=0)


def per_device(volume, cotangent, master, moment, second):
    planes = volume.shape[1]
    rows = volume.shape[2]
    cols = volume.shape[3]
    width = volume.shape[4]
    kernel = lax.all_gather(master.astype(jnp.bfloat16), "dp", axis=0, tiled=True).reshape(
        27, width, width
    )
    wide = with_halo(volume, (("spatial", 1),), 1)[0]
    padded = pad_sides(wide)
    preact = forward_taps(padded, kernel, planes, rows, cols)
    activated = jax.nn.silu(preact).astype(jnp.bfloat16)
    hidden_grad = (cotangent[0].reshape(-1, width).astype(jnp.float32) * silu_slope(preact)).astype(
        jnp.bfloat16
    )
    grad_block = hidden_grad.reshape(1, planes, rows, cols, width)
    wide_grad = with_halo(grad_block, (("spatial", 1),), 1)[0]
    grad_pad = pad_sides(wide_grad)
    input_grad = backward_taps(grad_pad, kernel, planes, rows, cols).astype(jnp.bfloat16)
    local_grad = weight_taps(padded, hidden_grad, planes, rows, cols)
    partial_grad = lax.psum_scatter(
        local_grad.astype(jnp.bfloat16), "dp", scatter_dimension=0, tiled=True
    ).astype(jnp.float32)
    shard = lax.psum(partial_grad, "spatial")
    cells_all = lax.axis_size("dp") * lax.axis_size("spatial") * planes * rows * cols
    weight_grad = shard / math.sqrt(cells_all)
    moment_next = 0.9 * moment + 0.1 * weight_grad
    second_next = 0.999 * second + 0.001 * weight_grad * weight_grad
    master_next = master - 0.001 * (moment_next / (jnp.sqrt(second_next) + 1e-08) + 0.01 * master)
    activation = activated.reshape(1, planes, rows, cols, width)
    input_block = input_grad.reshape(1, planes, rows, cols, width)
    return (activation, input_block, master_next, moment_next, second_next)


def solution(mesh):
    return jax.shard_map(
        per_device,
        mesh=mesh,
        in_specs=(
            P("dp", "spatial", None, None, None),
            P("dp", "spatial", None, None, None),
            P("dp", None),
            P("dp", None),
            P("dp", None),
        ),
        out_specs=(
            P("dp", "spatial", None, None, None),
            P("dp", "spatial", None, None, None),
            P("dp", None),
            P("dp", None),
            P("dp", None),
        ),
        check_vma=False,
    )
```

profile of v0, /device:TPU:0, one launch (start us, length us, event | category | flops | bytes accessed | tf_op | source)
XLA Modules:
  0.0 116.7 jit_solution(8562241958036103037)
XLA Ops:
  7.2 0.8 fusion.95
  8.0 2.4 %collective-permute-start = (bf16[1,1,16,8,128]{4,3,2,1,0:T(8,128)(2,1)S(1)}, bf16[1,1,16,8,128]{4,3,2,1,0:T(8,128)(2,1)S(1)}, u32[]{:S(2)}, u32[]{:S(2)}) collective-permute-start(bf16[1,1,16,8,128]{4,3,2,1,0:T(8,128)(2,1)S(1)} %get-tuple-element.64), channel_id=1, source_target_pairs={{0,1},{1,2},{2,3},{3,4},{4,5},{5,6},{6,7},{8,9},{9,10},{10,11},{11... | collective-permute-start | bytes 98312 | tf_op jit(solution)/shard_map/ppermute | solution.py:13
  10.4 1.3 %collective-permute-start.1 = (bf16[1,1,16,8,128]{4,3,2,1,0:T(8,128)(2,1)S(1)}, bf16[1,1,16,8,128]{4,3,2,1,0:T(8,128)(2,1)S(1)}, u32[]{:S(2)}, u32[]{:S(2)}) collective-permute-start(bf16[1,1,16,8,128]{4,3,2,1,0:T(8,128)(2,1)S(1)} %get-tuple-element.65), channel_id=1, source_target_pairs={{1,0},{2,1},{3,2},{4,3},{5,4},{6,5},{7,6},{9,8},{10,9},{11,10},{12... | collective-permute-start | bytes 98312 | tf_op jit(solution)/shard_map/ppermute | solution.py:16
  11.7 1.0 convert_element_type.25
  12.7 14.2 %all_gather.3 = bf16[3456,128]{1,0:T(8,128)(2,1)S(1)} all-gather(bf16[864,128]{1,0:T(8,128)(2,1)S(1)} %convert_element_type.25), channel_id=1, replica_groups=mesh['dp'=4,'spatial'=8] {'dp'}, dimensions={0}, use_global_device_ids=true | all-gather | bytes 1105920 | tf_op jit(solution)/shard_map/all_gather | solution.py:96
  31.2 0.7 copy-done.5
  31.9 0.8 fusion.33
  32.9 0.2 fusion.29
  33.1 0.2 fusion.28
  33.4 0.2 fusion.27
  33.6 0.2 fusion.26
  34.2 0.2 fusion.23
  34.8 0.2 fusion.20
  35.0 0.2 fusion.19
  35.4 0.2 fusion.32
  36.9 0.2 fusion.11
  38.2 2.4 %collective-permute-start.2 = (bf16[1,1,16,8,128]{4,3,2,1,0:T(8,128)(2,1)S(1)}, bf16[1,1,16,8,128]{4,3,2,1,0:T(8,128)(2,1)S(1)}, u32[]{:S(2)}, u32[]{:S(2)}) collective-permute-start(bf16[1,1,16,8,128]{4,3,2,1,0:T(8,128)(2,1)S(1)} %get-tuple-element.60), channel_id=1, source_target_pairs={{0,1},{1,2},{2,3},{3,4},{4,5},{5,6},{6,7},{8,9},{9,10},{10,11},{11... | collective-permute-start | bytes 98312 | tf_op jit(solution)/shard_map/ppermute | solution.py:13
  40.6 1.3 %collective-permute-start.3 = (bf16[1,1,16,8,128]{4,3,2,1,0:T(8,128)(2,1)S(1)}, bf16[1,1,16,8,128]{4,3,2,1,0:T(8,128)(2,1)S(1)}, u32[]{:S(2)}, u32[]{:S(2)}) collective-permute-start(bf16[1,1,16,8,128]{4,3,2,1,0:T(8,128)(2,1)S(1)} %get-tuple-element.61), channel_id=1, source_target_pairs={{1,0},{2,1},{3,2},{4,3},{5,4},{6,5},{7,6},{9,8},{10,9},{11,10},{12... | collective-permute-start | bytes 98312 | tf_op jit(solution)/shard_map/ppermute | solution.py:16
  42.1 0.9 copy-done.2
  43.0 3.1 %collective-permute-done.3 = bf16[1,1,16,8,128]{4,3,2,1,0:T(8,128)(2,1)S(1)} collective-permute-done((bf16[1,1,16,8,128]{4,3,2,1,0:T(8,128)(2,1)S(1)}, bf16[1,1,16,8,128]{4,3,2,1,0:T(8,128)(2,1)S(1)}, u32[]{:S(2)}, u32[]{:S(2)}) %collective-permute-start.3) | collective-permute-done | bytes 32800 | tf_op jit(solution)/shard_map/ppermute | solution.py:16
  50.9 0.8 fusion.4
  51.7 22.4 %reduce-scatter.2.cloned.1.call-done = bf16[864,128]{1,0:T(8,128)(2,1)} async-done(((bf16[3456,128]{1,0:T(8,128)(2,1)}), bf16[864,128]{1,0:T(8,128)(2,1)}) %reduce-scatter.2.cloned.1.call-update) | async-done | bytes 221200 | tf_op jit(solution)/shard_map/reduce_scatter | solution.py:111
  74.1 34.5 %all-reduce.3 = f32[864,128]{1,0:T(8,128)S(1)} all-reduce(bf16[864,128]{1,0:T(8,128)(2,1)} %reduce-scatter.2.cloned.1.call-done), channel_id=1, replica_groups=mesh['dp'=4,'spatial'=8] {'spatial'}, use_global_device_ids=true, to_apply=%region_1.2 | all-reduce | flops 110592 | bytes 663552 | tf_op jit(solution)/shard_map/psum | solution.py:114
  108.7 1.2 %multiply_subtract_fusion = (f32[864,128]{1,0:T(8,128)}, f32[864,128]{1,0:T(8,128)}, f32[864,128]{1,0:T(8,128)}) fusion(f32[864,128]{1,0:T(8,128)S(1)} %copy-done, f32[864,128]{1,0:T(8,128)S(1)} %all-reduce.3, f32[864,128]{1,0:T(8,128)S(1)} %copy-done.3, f32[864,128]{1,0:T(8,128)S(1)} %copy-done.4), kind=kLoop, calls=%fused_computation.156 | loop fusion | flops 1548288 | bytes 3096576 | tf_op jit(solution)/shard_map/sub | solution.py:119
  (94 shorter events, 12.4 us)
Async XLA Ops:
  7.2 66.9 %reduce-scatter.2.cloned.1.call-start = ((), (), s32[]{:S(2)}) async-start(), calls=%async_computation.1 | async-start | bytes 1105920 | tf_op jit(solution)/shard_map/reduce_scatter | solution.py:111
  8.0 18.9 %collective-permute-start = (bf16[1,1,16,8,128]{4,3,2,1,0:T(8,128)(2,1)S(1)}, bf16[1,1,16,8,128]{4,3,2,1,0:T(8,128)(2,1)S(1)}, u32[]{:S(2)}, u32[]{:S(2)}) collective-permute-start(bf16[1,1,16,8,128]{4,3,2,1,0:T(8,128)(2,1)S(1)} %get-tuple-element.64), channel_id=1, source_target_pairs={{0,1},{1,2},{2,3},{3,4},{4,5},{5,6},{6,7},{8,9},{9,10},{10,11},{11... | collective-permute-start | bytes 98312 | tf_op jit(solution)/shard_map/ppermute | solution.py:13
  10.4 16.5 %collective-permute-start.1 = (bf16[1,1,16,8,128]{4,3,2,1,0:T(8,128)(2,1)S(1)}, bf16[1,1,16,8,128]{4,3,2,1,0:T(8,128)(2,1)S(1)}, u32[]{:S(2)}, u32[]{:S(2)}) collective-permute-start(bf16[1,1,16,8,128]{4,3,2,1,0:T(8,128)(2,1)S(1)} %get-tuple-element.65), channel_id=1, source_target_pairs={{1,0},{2,1},{3,2},{4,3},{5,4},{6,5},{7,6},{9,8},{10,9},{11,10},{12... | collective-permute-start | bytes 98312 | tf_op jit(solution)/shard_map/ppermute | solution.py:16
  12.7 14.2 %copy-start.1 = (bf16[1,2,16,8,128]{4,3,2,1,0:T(8,128)(2,1)S(1)}, bf16[1,2,16,8,128]{4,3,2,1,0:T(8,128)(2,1)}, u32[]{:S(2)}) copy-start(bf16[1,2,16,8,128]{4,3,2,1,0:T(8,128)(2,1)} %param.5) | copy-start | bytes 196612
  31.1 0.8 copy-start.5
  38.2 4.8 %collective-permute-start.2 = (bf16[1,1,16,8,128]{4,3,2,1,0:T(8,128)(2,1)S(1)}, bf16[1,1,16,8,128]{4,3,2,1,0:T(8,128)(2,1)S(1)}, u32[]{:S(2)}, u32[]{:S(2)}) collective-permute-start(bf16[1,1,16,8,128]{4,3,2,1,0:T(8,128)(2,1)S(1)} %get-tuple-element.60), channel_id=1, source_target_pairs={{0,1},{1,2},{2,3},{3,4},{4,5},{5,6},{6,7},{8,9},{9,10},{10,11},{11... | collective-permute-start | bytes 98312 | tf_op jit(solution)/shard_map/ppermute | solution.py:13
  40.6 5.6 %collective-permute-start.3 = (bf16[1,1,16,8,128]{4,3,2,1,0:T(8,128)(2,1)S(1)}, bf16[1,1,16,8,128]{4,3,2,1,0:T(8,128)(2,1)S(1)}, u32[]{:S(2)}, u32[]{:S(2)}) collective-permute-start(bf16[1,1,16,8,128]{4,3,2,1,0:T(8,128)(2,1)S(1)} %get-tuple-element.61), channel_id=1, source_target_pairs={{1,0},{2,1},{3,2},{4,3},{5,4},{6,5},{7,6},{9,8},{10,9},{11,10},{12... | collective-permute-start | bytes 98312 | tf_op jit(solution)/shard_map/ppermute | solution.py:16
  42.1 0.9 copy-start.2
  50.5 58.1 %copy-start.4 = (f32[864,128]{1,0:T(8,128)S(1)}, f32[864,128]{1,0:T(8,128)}, u32[]{:S(2)}) copy-start(f32[864,128]{1,0:T(8,128)} %param.8) | copy-start | bytes 1327108
  50.9 57.8 %copy-start = (f32[864,128]{1,0:T(8,128)S(1)}, f32[864,128]{1,0:T(8,128)}, u32[]{:S(2)}) copy-start(f32[864,128]{1,0:T(8,128)} %param.7) | copy-start | bytes 1327108
  50.9 57.8 %copy-start.3 = (f32[864,128]{1,0:T(8,128)S(1)}, f32[864,128]{1,0:T(8,128)}, u32[]{:S(2)}) copy-start(f32[864,128]{1,0:T(8,128)} %param.9) | copy-start | bytes 1327108
Sparse Core Ops, SparseCore 0:
  43.1 30.9 reduce-scatter.1
where the time goes:
time: 117 us
  blocking collectives  48.7 us (42%)
  waiting for transfers between devices  25.6 us (22%)
  matrix products  15.3 us (13%)
  between operations  14.6 us (12%)
  starting transfers between devices  7.38 us (6%)
  local copies, waits for them, and re-layouts  2.93 us (3%)
  other arithmetic  2.34 us (2%)
    psum x1, blocking collectives, per_device(): shard = lax.psum(partial_grad, 'spatial')  34.5 us
    reduce_scatter x1, waiting for transfers between devices, per_device(): lax.psum_scatter(local_grad.astype(jnp.bfloat16), 'dp', scatter_dimension...  22.4 us
    all_gather x1, blocking collectives, per_device(): lax.all_gather(master.astype(jnp.bfloat16), 'dp', axis=0, tiled=True)  14.2 us
    dot_general x27, matrix products, weight_taps(): lax.dot_general(piece, hidden_grad, (((0,), (0,)), ((), ())), preferred_e...  5.53 us
    dot_general x27, matrix products, backward_taps(): lax.dot_general(piece, kernel[tap_index], (((1,), (1,)), ((), ())), prefe...  5.07 us
    ppermute x2, starting transfers between devices, with_halo(): lax.ppermute(lax.slice_in_dim(block, block.shape[dim] - width, None, axis...  4.76 us
    dot_general x27, matrix products, forward_taps(): jnp.dot(piece, kernel[tap_index], preferred_element_type=jnp.float32)  4.67 us
    ppermute x2, waiting for transfers between devices, with_halo(): lax.ppermute(lax.slice_in_dim(block, 0, width, axis=dim), axis, backward)  3.13 us
  transfers between devices with their start and end apart: 5, of which 2 were waited for; matrix products, arithmetic and copies ran while one was open for 6% of the time, Pallas kernels for 0%

commit v1 on v0

--- a/solution.py
+++ b/solution.py
@@ -111,7 +111,7 @@
     partial_grad = lax.psum_scatter(
         local_grad.astype(jnp.bfloat16), "dp", scatter_dimension=0, tiled=True
     ).astype(jnp.float32)
-    shard = lax.psum(partial_grad, "spatial")
+    shard = jnp.sum(lax.all_gather(partial_grad, "spatial"), axis=0)
     cells_all = lax.axis_size("dp") * lax.axis_size("spatial") * planes * rows * cols
     weight_grad = shard / math.sqrt(cells_all)
     moment_next = 0.9 * moment + 0.1 * weight_grad

time: 117 us -> 123 us (1.051)
  blocking collectives: 48.7 us -> 15.7 us
  waiting for transfers between devices: 25.6 us -> 58.4 us
  other arithmetic: 2.34 us -> 7.12 us
  starting transfers between devices: 7.38 us -> 8.72 us
    all_gather x0 -> x1, waiting for transfers between devices: none -> 36.8 us  [per_device(): shard = jnp.sum(lax.all_gather(partial_grad, 'spatial'), axis=0)]
    psum x1 -> x0, blocking collectives: 34.5 us -> none  [per_device(): shard = lax.psum(partial_grad, 'spatial')]
    ppermute x2, waiting for transfers between devices: 3.13 us -> 0.01 us  [with_halo(): lax.ppermute(lax.slice_in_dim(block, 0, width, axis=dim), axis, backward)]
    reduce_sum x0 -> x1, other arithmetic: none -> 2.22 us  [per_device(): shard = jnp.sum(lax.all_gather(partial_grad, 'spatial'), axis=0)]
    all_gather x0 -> x1, other arithmetic: none -> 1.73 us  [per_device(): shard = jnp.sum(lax.all_gather(partial_grad, 'spatial'), axis=0)]
    reduce_scatter x1, waiting for transfers between devices: 22.4 us -> 20.8 us  [per_device(): lax.psum_scatter(local_grad.astype(jnp.bfloat16), 'dp', scatter_dimension...]
    all_gather x1, blocking collectives: 14.2 us -> 15.7 us  [per_device(): lax.all_gather(master.astype(jnp.bfloat16), 'dp', axis=0, tiled=True)]
    ppermute x2, starting transfers between devices: 4.76 us -> 6.06 us  [with_halo(): lax.ppermute(lax.slice_in_dim(block, block.shape[dim] - width, None, axis...]
  transfers between devices with their start and end apart: 5 -> 6, of which waited for: 2 -> 3; matrix products, arithmetic and copies ran while one was open for 6% -> 5% of each run, Pallas kernels for 0% -> 0%
where the time goes in v1:
time: 123 us; the launch traced here: 122 us
  waiting for transfers between devices  58.4 us (47%)
  blocking collectives  15.7 us (13%)
  matrix products  15.3 us (12%)
  between operations  14.6 us (12%)
  starting transfers between devices  8.72 us (7%)
  other arithmetic  7.12 us (6%)
  local copies, waits for them, and re-layouts  2.26 us (2%)
    all_gather x1, waiting for transfers between devices, per_device(): shard = jnp.sum(lax.all_gather(partial_grad, 'spatial'), axis=0)  36.8 us
    reduce_scatter x1, waiting for transfers between devices, per_device(): lax.psum_scatter(local_grad.astype(jnp.bfloat16), 'dp', scatter_dimension...  20.8 us
    all_gather x1, blocking collectives, per_device(): lax.all_gather(master.astype(jnp.bfloat16), 'dp', axis=0, tiled=True)  15.7 us
    ppermute x2, starting transfers between devices, with_halo(): lax.ppermute(lax.slice_in_dim(block, block.shape[dim] - width, None, axis...  6.06 us
    dot_general x27, matrix products, weight_taps(): lax.dot_general(piece, hidden_grad, (((0,), (0,)), ((), ())), preferred_e...  5.53 us
    dot_general x27, matrix products, backward_taps(): lax.dot_general(piece, kernel[tap_index], (((1,), (1,)), ((), ())), prefe...  5.07 us
    dot_general x27, matrix products, forward_taps(): jnp.dot(piece, kernel[tap_index], preferred_element_type=jnp.float32)  4.68 us
    ppermute x2, starting transfers between devices, with_halo(): lax.ppermute(lax.slice_in_dim(block, 0, width, axis=dim), axis, backward)  2.57 us
  transfers between devices with their start and end apart: 6, of which 3 were waited for; matrix products, arithmetic and copies ran while one was open for 5% of the time, Pallas kernels for 0%

profile of v1, /device:TPU:0, one launch (start us, length us, event | category | flops | bytes accessed | tf_op | source)
XLA Modules:
  0.0 122.1 jit_solution(16091689794086015704)
XLA Ops:
  7.2 0.8 fusion.95
  8.0 1.3 %collective-permute-start.1 = (bf16[1,1,16,8,128]{4,3,2,1,0:T(8,128)(2,1)S(1)}, bf16[1,1,16,8,128]{4,3,2,1,0:T(8,128)(2,1)S(1)}, u32[]{:S(2)}, u32[]{:S(2)}) collective-permute-start(bf16[1,1,16,8,128]{4,3,2,1,0:T(8,128)(2,1)S(1)} %get-tuple-element.65), channel_id=1, source_target_pairs={{1,0},{2,1},{3,2},{4,3},{5,4},{6,5},{7,6},{9,8},{10,9},{11,10},{12... | collective-permute-start | bytes 98312 | tf_op jit(solution)/shard_map/ppermute | solution.py:16
  9.3 3.0 %collective-permute-start = (bf16[1,1,16,8,128]{4,3,2,1,0:T(8,128)(2,1)S(1)}, bf16[1,1,16,8,128]{4,3,2,1,0:T(8,128)(2,1)S(1)}, u32[]{:S(2)}, u32[]{:S(2)}) collective-permute-start(bf16[1,1,16,8,128]{4,3,2,1,0:T(8,128)(2,1)S(1)} %get-tuple-element.64), channel_id=1, source_target_pairs={{0,1},{1,2},{2,3},{3,4},{4,5},{5,6},{6,7},{8,9},{9,10},{10,11},{11... | collective-permute-start | bytes 98312 | tf_op jit(solution)/shard_map/ppermute | solution.py:13
  12.3 1.0 convert_element_type.23
  13.4 15.7 %all_gather.12 = bf16[3456,128]{1,0:T(8,128)(2,1)S(1)} all-gather(bf16[864,128]{1,0:T(8,128)(2,1)S(1)} %convert_element_type.23), channel_id=1, replica_groups=mesh['dp'=4,'spatial'=8] {'dp'}, dimensions={0}, use_global_device_ids=true | all-gather | bytes 1105920 | tf_op jit(solution)/shard_map/all_gather | solution.py:96
  29.1 0.9 maximum_bitcast_fusion
  34.3 0.8 fusion.33
  35.3 0.2 fusion.29
  35.7 0.2 fusion.27
  35.9 0.2 fusion.26
  36.6 0.2 fusion.23
  37.4 0.2 fusion.19
  37.8 0.2 fusion.32
  39.3 0.2 fusion.11
  40.8 0.9 copy-done.2
  41.8 1.3 %collective-permute-start.3 = (bf16[1,1,16,8,128]{4,3,2,1,0:T(8,128)(2,1)S(1)}, bf16[1,1,16,8,128]{4,3,2,1,0:T(8,128)(2,1)S(1)}, u32[]{:S(2)}, u32[]{:S(2)}) collective-permute-start(bf16[1,1,16,8,128]{4,3,2,1,0:T(8,128)(2,1)S(1)} %get-tuple-element.61), channel_id=1, source_target_pairs={{1,0},{2,1},{3,2},{4,3},{5,4},{6,5},{7,6},{9,8},{10,9},{11,10},{12... | collective-permute-start | bytes 98312 | tf_op jit(solution)/shard_map/ppermute | solution.py:16
  43.1 3.0 %collective-permute-start.2 = (bf16[1,1,16,8,128]{4,3,2,1,0:T(8,128)(2,1)S(1)}, bf16[1,1,16,8,128]{4,3,2,1,0:T(8,128)(2,1)S(1)}, u32[]{:S(2)}, u32[]{:S(2)}) collective-permute-start(bf16[1,1,16,8,128]{4,3,2,1,0:T(8,128)(2,1)S(1)} %get-tuple-element.60), channel_id=1, source_target_pairs={{0,1},{1,2},{2,3},{3,4},{4,5},{5,6},{6,7},{8,9},{9,10},{10,11},{11... | collective-permute-start | bytes 98312 | tf_op jit(solution)/shard_map/ppermute | solution.py:13
  46.1 0.8 collective-permute-done.2
  47.2 20.8 %reduce-scatter.2.cloned.1.call-done = bf16[864,128]{1,0:T(8,128)(2,1)} async-done(((bf16[3456,128]{1,0:T(8,128)(2,1)}), bf16[864,128]{1,0:T(8,128)(2,1)}) %reduce-scatter.2.cloned.1.call-update) | async-done | bytes 221200 | tf_op jit(solution)/shard_map/reduce_scatter | solution.py:111
  68.0 1.7 %all_gather.16 = f32[864,128]{1,0:T(8,128)} convert(bf16[864,128]{1,0:T(8,128)(2,1)} %reduce-scatter.2.cloned.1.call-done) | non-fusion elementwise | flops 110592 | bytes 663552 | tf_op jit(solution)/shard_map/all_gather | solution.py:114
  74.2 0.8 fusion.4
  75.0 36.8 %all-gather.3.cloned.1.call-done = f32[6912,128]{1,0:T(8,128)} async-done(((f32[864,128]{1,0:T(8,128)}), f32[6912,128]{1,0:T(8,128)}) %all-gather.3.cloned.1.call-update) | async-done | bytes 3538960 | tf_op jit(solution)/shard_map/all_gather | solution.py:114
  111.8 2.2 %reduce_sum.9 = f32[864,128]{1,0:T(8,128)S(1)} reduce(f32[8,864,128]{2,1,0:T(8,128)} %bitcast.179, f32[]{:T(128)} %constant.8.clone.1), dimensions={0}, to_apply=%region_1.2 | reduce | flops 774144 | bytes 3981316 | tf_op jit(solution)/shard_map/reduce_sum | solution.py:114
  114.0 1.2 %multiply_subtract_fusion = (f32[864,128]{1,0:T(8,128)}, f32[864,128]{1,0:T(8,128)}, f32[864,128]{1,0:T(8,128)}) fusion(f32[864,128]{1,0:T(8,128)S(1)} %copy-done, f32[864,128]{1,0:T(8,128)S(1)} %reduce_sum.9, f32[864,128]{1,0:T(8,128)S(1)} %copy-done.3, f32[864,128]{1,0:T(8,128)S(1)} %copy-done.4), kind=kLoop, calls=%fused_computation.156 | loop fusion | flops 1548288 | bytes 3096576 | tf_op jit(solution)/shard_map/sub | solution.py:119
  (98 shorter events, 12.9 us)
Async XLA Ops:
  7.2 24.0 %copy-start.1 = (bf16[1,2,16,8,128]{4,3,2,1,0:T(8,128)(2,1)S(1)}, bf16[1,2,16,8,128]{4,3,2,1,0:T(8,128)(2,1)}, u32[]{:S(2)}) copy-start(bf16[1,2,16,8,128]{4,3,2,1,0:T(8,128)(2,1)} %param.5) | copy-start | bytes 196612
  7.2 60.8 %reduce-scatter.2.cloned.1.call-start = ((), (), s32[]{:S(2)}) async-start(), calls=%async_computation.1 | async-start | bytes 1105920 | tf_op jit(solution)/shard_map/reduce_scatter | solution.py:111
  8.0 21.1 %collective-permute-start.1 = (bf16[1,1,16,8,128]{4,3,2,1,0:T(8,128)(2,1)S(1)}, bf16[1,1,16,8,128]{4,3,2,1,0:T(8,128)(2,1)S(1)}, u32[]{:S(2)}, u32[]{:S(2)}) collective-permute-start(bf16[1,1,16,8,128]{4,3,2,1,0:T(8,128)(2,1)S(1)} %get-tuple-element.65), channel_id=1, source_target_pairs={{1,0},{2,1},{3,2},{4,3},{5,4},{6,5},{7,6},{9,8},{10,9},{11,10},{12... | collective-permute-start | bytes 98312 | tf_op jit(solution)/shard_map/ppermute | solution.py:16
  9.3 19.8 %collective-permute-start = (bf16[1,1,16,8,128]{4,3,2,1,0:T(8,128)(2,1)S(1)}, bf16[1,1,16,8,128]{4,3,2,1,0:T(8,128)(2,1)S(1)}, u32[]{:S(2)}, u32[]{:S(2)}) collective-permute-start(bf16[1,1,16,8,128]{4,3,2,1,0:T(8,128)(2,1)S(1)} %get-tuple-element.64), channel_id=1, source_target_pairs={{0,1},{1,2},{2,3},{3,4},{4,5},{5,6},{6,7},{8,9},{9,10},{10,11},{11... | collective-permute-start | bytes 98312 | tf_op jit(solution)/shard_map/ppermute | solution.py:13
  31.4 2.9 %copy-start.5 = (bf16[1,2,16,8,128]{4,3,2,1,0:T(8,128)(2,1)S(1)}, bf16[1,2,16,8,128]{4,3,2,1,0:T(8,128)(2,1)}, u32[]{:S(2)}) copy-start(bf16[1,2,16,8,128]{4,3,2,1,0:T(8,128)(2,1)} %param.6) | copy-start | bytes 196612
  40.8 0.9 copy-start.2
  41.7 70.1 %all-gather.3.cloned.1.call-start = ((), (), s32[]{:S(2)}) async-start(), calls=%async_computation.2 | async-start | bytes 3981312 | tf_op jit(solution)/shard_map/all_gather | solution.py:114
  41.8 4.3 %collective-permute-start.3 = (bf16[1,1,16,8,128]{4,3,2,1,0:T(8,128)(2,1)S(1)}, bf16[1,1,16,8,128]{4,3,2,1,0:T(8,128)(2,1)S(1)}, u32[]{:S(2)}, u32[]{:S(2)}) collective-permute-start(bf16[1,1,16,8,128]{4,3,2,1,0:T(8,128)(2,1)S(1)} %get-tuple-element.61), channel_id=1, source_target_pairs={{1,0},{2,1},{3,2},{4,3},{5,4},{6,5},{7,6},{9,8},{10,9},{11,10},{12... | collective-permute-start | bytes 98312 | tf_op jit(solution)/shard_map/ppermute | solution.py:16
  43.1 3.9 %collective-permute-start.2 = (bf16[1,1,16,8,128]{4,3,2,1,0:T(8,128)(2,1)S(1)}, bf16[1,1,16,8,128]{4,3,2,1,0:T(8,128)(2,1)S(1)}, u32[]{:S(2)}, u32[]{:S(2)}) collective-permute-start(bf16[1,1,16,8,128]{4,3,2,1,0:T(8,128)(2,1)S(1)} %get-tuple-element.60), channel_id=1, source_target_pairs={{0,1},{1,2},{2,3},{3,4},{4,5},{5,6},{6,7},{8,9},{9,10},{10,11},{11... | collective-permute-start | bytes 98312 | tf_op jit(solution)/shard_map/ppermute | solution.py:13
  73.0 41.0 %copy-start = (f32[864,128]{1,0:T(8,128)S(1)}, f32[864,128]{1,0:T(8,128)}, u32[]{:S(2)}) copy-start(f32[864,128]{1,0:T(8,128)} %param.7) | copy-start | bytes 1327108
  73.0 41.0 %copy-start.3 = (f32[864,128]{1,0:T(8,128)S(1)}, f32[864,128]{1,0:T(8,128)}, u32[]{:S(2)}) copy-start(f32[864,128]{1,0:T(8,128)} %param.9) | copy-start | bytes 1327108
  73.0 41.0 %copy-start.4 = (f32[864,128]{1,0:T(8,128)S(1)}, f32[864,128]{1,0:T(8,128)}, u32[]{:S(2)}) copy-start(f32[864,128]{1,0:T(8,128)} %param.8) | copy-start | bytes 1327108
Sparse Core Ops, SparseCore 0:
  41.8 26.1 reduce-scatter.1
  70.2 41.5 all-gather.2
